TPU v7x, 512 devices: a whole 4x4x16 slice. The times are simulated.
512 devices in a mesh: frames: 32 (over y, x, core), heads: 16 (over z).
Axes of the slice: x: 4, y: 4, z: 16, core: 2. Of those that a mesh axis runs over, the one named last changes fastest.
Arguments:
- frames: bfloat16 [32768, 1152], P('frames', 'heads'), may hold values from -6 to 6
- latents: bfloat16 [256, 1152], P('frames'), may hold values from -400 to 400
- w_query: bfloat16 [1152, 4096], P(None, 'heads'), may hold values from -0.1875 to 0.1875
- w_key: bfloat16 [1152, 4096], P(None, 'heads'), may hold values from -0.1875 to 0.1875
- w_value: bfloat16 [1152, 4096], P(None, 'heads'), may hold values from -0.1875 to 0.1875
- w_out: bfloat16 [4096, 8192], P('heads', 'frames'), may hold values from -0.09375 to 0.09375
- norm_gain: float32 [8192], P('frames'), may hold values from 0.5 to 1.5
- w_gate: bfloat16 [8192, 16384], P('frames', 'heads'), may hold values from -0.0625 to 0.0625
- w_up: bfloat16 [8192, 16384], P('frames', 'heads'), may hold values from -0.0625 to 0.0625
- w_down: bfloat16 [16384, 8192], P('heads', 'frames'), may hold values from -0.046875 to 0.046875
Outputs:
- block_out: bfloat16 [256, 8192], P('heads', 'frames')
All inputs are finite; a program needn't handle non-finite values.
Results may differ from a plain program's by a relative error of at most 0.023.
Values may be sent and summed in bfloat16 or wider, within the bound.
No kernel may reach another device: no remote copies, remote signals or barrier semaphores. Data moves between devices by JAX's collectives and lax.ppermute only.
A program may use at most 64 MiB of HBM per device.

v0:
```python
import jax
import jax.numpy as jnp
from jax import lax
from jax.sharding import Mesh
from jax.sharding import PartitionSpec as P

HDIM = 128
D = 8192
FRAMES = ("frames_0", "frames_1", "frames_2")
BF16 = jnp.bfloat16
F32 = jnp.float32
norm_eps = 1e-06


def exchange(blocks, axis):
    return lax.all_to_all(blocks, axis, split_axis=0, concat_axis=0, tiled=True)


def collect_rows(array, axis):
    peers = lax.axis_size(axis)
    blocks = exchange(jnp.broadcast_to(array[None], (peers, *array.shape)), axis)
    return blocks.reshape(peers * array.shape[0], *array.shape[1:])


def sum_rows_at_owner(array, axis):
    peers = lax.axis_size(axis)
    blocks = array.astype(BF16).reshape(peers, array.shape[0] // peers, *array.shape[1:])
    return jnp.sum(exchange(blocks, axis).astype(F32), axis=0)


def split_terms(array, count):
    terms = []
    for _ in range(count):
        term = lax.reduce_precision(array, 8, 7)
        terms.append(term.astype(BF16))
        array = array - term
    return terms


def joined_terms(terms):
    array = terms[-1].astype(F32)
    for term in terms[-2::-1]:
        array = array + term.astype(F32)
    return array


def merged_softmax(local_max, total, mixed):
    peers = lax.axis_size(FRAMES)
    rows, heads = local_max.shape
    share = rows // peers
    terms = jnp.stack(split_terms(local_max, 3) + split_terms(total, 3), axis=-1)
    stats = terms.reshape(peers, share * heads * 6)
    stats = jnp.pad(stats, ((0, 0), (0, -stats.shape[1] % HDIM))).reshape(peers, -1, HDIM)
    body = mixed.astype(BF16).reshape(peers, share * heads, HDIM)
    arrived = exchange(jnp.concatenate([body, stats], axis=1), FRAMES)
    body = arrived[:, : share * heads].reshape(peers, share, heads, HDIM).astype(F32)
    stats = arrived[:, share * heads :].reshape(peers, -1)[:, : share * heads * 6]
    stats = stats.reshape(peers, share, heads, 6)
    part_max = joined_terms([stats[..., k] for k in range(3)])
    part_total = joined_terms([stats[..., k] for k in range(3, 6)])
    scale = jnp.exp(part_max - jnp.max(part_max, axis=0))
    total = jnp.sum(part_total * scale, axis=0)
    mixed = jnp.sum(body * scale[..., None], axis=0)
    return (mixed / total[..., None]).reshape(share, heads * HDIM).astype(BF16)


def on_device(frames, latents, w_query, w_key, w_value, w_out, norm_gain, w_gate, w_up, w_down):
    local_query = jnp.dot(latents, w_query, preferred_element_type=F32).astype(BF16)
    queries = collect_rows(local_query, FRAMES)
    width = w_key.shape[1]
    piece = lax.all_gather(frames, "heads", axis=1, tiled=True)
    keys = jnp.dot(piece, w_key, preferred_element_type=F32)
    values = jnp.dot(piece, w_value, preferred_element_type=F32)
    heads_here = width // HDIM
    latent_count = queries.shape[0]
    query_heads = queries.reshape(latent_count, heads_here, HDIM)
    key_heads = keys.astype(BF16).reshape(-1, heads_here, HDIM)
    value_heads = values.astype(BF16).reshape(-1, heads_here, HDIM)
    scores = jnp.einsum(
        "qhd,khd->qhk", query_heads, key_heads, preferred_element_type=F32
    ) * HDIM ** (-0.5)
    local_max = jnp.max(scores, axis=2)
    weights = jnp.exp(scores - local_max[:, :, None])
    total = jnp.sum(weights, axis=2)
    mixed = jnp.einsum(
        "qhk,khd->qhd", weights.astype(BF16), value_heads, preferred_element_type=F32
    )
    attention = collect_rows(merged_softmax(local_max, total, mixed), FRAMES)
    latent_state = sum_rows_at_owner(
        jnp.dot(attention, w_out, preferred_element_type=F32), "heads"
    ).astype(BF16)
    latent_full = collect_rows(latent_state, "heads")
    full_float = latent_full.astype(F32)
    square_part = jnp.sum(full_float * full_float, axis=1)
    normed = (full_float * norm_gain[None, :]).astype(BF16)
    gate_part = jnp.dot(normed, w_gate, preferred_element_type=F32).astype(BF16)
    up_part = jnp.dot(normed, w_up, preferred_element_type=F32).astype(BF16)
    square_terms = jnp.stack(split_terms(square_part, 2), axis=1)
    square_terms = jnp.pad(square_terms, ((0, 0), (0, 126)))
    peers = lax.axis_size(FRAMES)
    packed = jnp.concatenate([gate_part, up_part, square_terms], axis=1)
    sums = jnp.sum(exchange(packed.reshape(peers, -1, packed.shape[1]), FRAMES).astype(F32), axis=0)
    units = w_gate.shape[1]
    gate_sum, up_sum = (sums[:, :units], sums[:, units : 2 * units])
    squares = sums[:, 2 * units : 2 * units + 1] + sums[:, 2 * units + 1 : 2 * units + 2]
    scale_rows = lax.rsqrt(squares / D + norm_eps)
    hidden = (jax.nn.silu(gate_sum * scale_rows) * (up_sum * scale_rows)).astype(BF16)
    hidden_full = collect_rows(hidden, FRAMES)
    down = sum_rows_at_owner(jnp.dot(hidden_full, w_down, preferred_element_type=F32), "heads")
    return (latent_state.astype(F32) + down).astype(BF16)


def solution(mesh):
    torus = Mesh(
        mesh.devices.reshape(4, 4, 2, mesh.shape["heads"]),
        ("frames_0", "frames_1", "frames_2", "heads"),
    )
    placed = (
        P(FRAMES, "heads"),
        P(FRAMES, None),
        P(None, "heads"),
        P(None, "heads"),
        P(None, "heads"),
        P("heads", FRAMES),
        P(FRAMES),
        P(FRAMES, "heads"),
        P(FRAMES, "heads"),
        P("heads", FRAMES),
    )
    return jax.shard_map(
        on_device, mesh=torus, in_specs=placed, out_specs=P("heads", FRAMES), check_vma=False
    )
```

profile of v0, /device:TPU:32, one launch (start us, length us, event | category | flops | bytes accessed | tf_op | source)
XLA Modules:
  0.0 226.5 jit_solution(6184290056534508303)
XLA Ops:
  6.5 0.7 all-gather.2.cloned.1.call-update
  7.3 1.3 convolution_convert_fusion.7
  8.6 14.9 %all_to_all.40 = bf16[32,8,256]{2,1,0:T(8,128)(2,1)S(1)} all-to-all(bf16[32,8,256]{2,1,0:T(8,128)(2,1)S(1)} %broadcast_in_dim.8), channel_id=1, replica_groups=mesh['frames_0'=4,'frames_1'=4,'frames_2'=2,'heads'=16] {'frames_0','fra..., dimensions={0} | all-to-all | bytes 262144 | tf_op jit(solution)/shard_map/all_to_all | solution.py:16
  23.5 63.2 %all-gather.2.cloned.1.call-done = bf16[1024,1152]{0,1:T(8,128)(2,1)} async-done(((bf16[1024,72]{0,1:T(8,128)(2,1)}), bf16[1024,1152]{0,1:T(8,128)(2,1)}) %all-gather.2.cloned.1.call-update) | async-done | bytes 2359312 | tf_op jit(solution)/shard_map/all_gather | solution.py:71
  86.7 2.5 %convolution_convert_fusion.2 = bf16[1024,256]{0,1:T(8,128)(2,1)S(1)} fusion(bf16[1024,1152]{0,1:T(8,128)(2,1)} %all-gather.2.cloned.1.call-done, bf16[1152,256]{1,0:T(8,128)(2,1)S(1)} %copy-done), kind=kOutput, calls=%fused_computation.10 | convolution fusion | flops 604241920 | bytes 3473408 | tf_op jit(solution)/shard_map/dot_general | solution.py:72
  89.3 0.0 copy-start.7
  89.3 0.5 bitcast_reduce_fusion
  89.8 0.4 fusion.2
  90.2 0.8 copy-done.6
  90.9 0.1 copy-done.7
  91.0 0.9 convolution_convert_fusion.3
  91.9 0.0 copy-start.4
  92.0 0.5 fusion.4
  92.5 0.0 copy-start.5
  92.5 0.0 copy-start.1
  92.5 0.1 copy.82
  92.7 0.2 copy.83
  92.9 0.2 reshape.184
  93.1 0.0 copy-start.2
  93.1 15.2 %all_to_all.41 = bf16[32,17,128]{2,1,0:T(8,128)(2,1)S(1)} all-to-all(bf16[32,17,128]{2,1,0:T(8,128)(2,1)S(1)} %pad_maximum_fusion), channel_id=1, replica_groups=mesh['frames_0'=4,'frames_1'=4,'frames_2'=2,'heads'=16] {'frames_0','fra..., dimensions={0} | all-to-all | bytes 278528 | tf_op jit(solution)/shard_map/all_to_all | solution.py:16
  108.3 0.1 copy.85
  108.5 0.1 fusion.32
  108.6 0.1 subtract_exponential_fusion
  108.7 0.2 fusion.20
  108.9 0.1 copy.91
  109.0 0.1 copy.86
  109.0 0.1 multiply_reduce_fusion.1
  109.2 0.1 fusion.19
  109.3 11.4 %all_to_all.42 = bf16[32,8,256]{2,1,0:T(8,128)(2,1)S(1)} all-to-all(bf16[32,8,256]{2,1,0:T(8,128)(2,1)S(1)} %broadcast_in_dim.9), channel_id=1, replica_groups=mesh['frames_0'=4,'frames_1'=4,'frames_2'=2,'heads'=16] {'frames_0','fra..., dimensions={0} | all-to-all | bytes 262144 | tf_op jit(solution)/shard_map/all_to_all | solution.py:16
  120.7 0.2 convolution_convert_fusion.5
  120.9 22.1 %all_to_all.43 = bf16[16,16,256]{2,1,0:T(8,128)(2,1)S(1)} all-to-all(bf16[16,16,256]{2,1,0:T(8,128)(2,1)S(1)} %bitcast.85), channel_id=1, replica_groups=mesh['frames_0'=4,'frames_1'=4,'frames_2'=2,'heads'=16] {'heads'}, dimensions={0} | all-to-all | bytes 262144 | tf_op jit(solution)/shard_map/all_to_all | solution.py:16
  143.1 19.1 %all_to_all.44 = bf16[16,16,256]{2,1,0:T(8,128)(2,1)S(1)} all-to-all(bf16[16,16,256]{2,1,0:T(8,128)(2,1)S(1)} %broadcast_in_dim.10), channel_id=1, replica_groups=mesh['frames_0'=4,'frames_1'=4,'frames_2'=2,'heads'=16] {'heads'}, dimensions={0} | all-to-all | bytes 262144 | tf_op jit(solution)/shard_map/all_to_all | solution.py:16
  162.2 0.1 multiply_reduce_fusion
  162.4 0.1 reduce_sum.79
  162.5 0.1 copy.92
  162.7 0.3 convolution_convert_fusion
  163.0 0.3 convolution_convert_fusion.1
  163.3 0.1 fusion.6
  163.4 0.0 copy-start.3
  163.4 22.0 %all_to_all.45 = bf16[32,8,2176]{2,1,0:T(8,128)(2,1)S(1)} all-to-all(bf16[32,8,2176]{2,1,0:T(8,128)(2,1)S(1)} %fusion.6), channel_id=1, replica_groups=mesh['frames_0'=4,'frames_1'=4,'frames_2'=2,'heads'=16] {'frames_0','fra..., dimensions={0} | all-to-all | bytes 2228224 | tf_op jit(solution)/shard_map/all_to_all | solution.py:16
  185.4 0.2 convert_reduce_fusion
  185.5 0.2 fusion.24
  185.7 0.1 fusion.16
  185.8 0.1 broadcast_in_dim.11
  185.9 15.0 %all_to_all.46 = bf16[32,8,1024]{2,1,0:T(8,128)(2,1)S(1)} all-to-all(bf16[32,8,1024]{2,1,0:T(8,128)(2,1)S(1)} %broadcast_in_dim.11), channel_id=1, replica_groups=mesh['frames_0'=4,'frames_1'=4,'frames_2'=2,'heads'=16] {'frames_0','fra..., dimensions={0} | all-to-all | bytes 1048576 | tf_op jit(solution)/shard_map/all_to_all | solution.py:16
  200.9 0.3 convolution_convert_fusion.4
  201.2 17.9 %all_to_all.47 = bf16[16,16,256]{2,1,0:T(8,128)(2,1)S(1)} all-to-all(bf16[16,16,256]{2,1,0:T(8,128)(2,1)S(1)} %bitcast.86), channel_id=1, replica_groups=mesh['frames_0'=4,'frames_1'=4,'frames_2'=2,'heads'=16] {'heads'}, dimensions={0} | all-to-all | bytes 262144 | tf_op jit(solution)/shard_map/all_to_all | solution.py:16
  219.1 0.6 add_convert_fusion
  (33 shorter events, 0.4 us)
Async XLA Ops:
  6.5 80.2 %copy-start = (bf16[1152,256]{1,0:T(8,128)(2,1)S(1)}, bf16[1152,256]{1,0:T(8,128)(2,1)}, u32[]{:S(2)}) copy-start(bf16[1152,256]{1,0:T(8,128)(2,1)} %param.13) | copy-start | bytes 1769476
  6.5 80.2 %all-gather.2.cloned.1.call-start = ((), (), s32[]{:S(2)}) async-start(), calls=%async_computation.8 | async-start | bytes 2506752 | tf_op jit(solution)/shard_map/all_gather | solution.py:71
  89.3 1.7 copy-start.6
  89.3 1.8 copy-start.7
  91.9 28.8 %copy-start.4 = (bf16[256,256]{1,0:T(8,128)(2,1)S(1)}, bf16[256,256]{1,0:T(8,128)(2,1)}, u32[]{:S(2)}) copy-start(bf16[256,256]{1,0:T(8,128)(2,1)} %param.15) | copy-start | bytes 393220
  92.5 70.1 %copy-start.5 = (f32[256]{0:T(256)S(1)}, f32[256]{0:T(256)}, u32[]{:S(2)}) copy-start(f32[256]{0:T(256)} %param.16) | copy-start | bytes 3076
  92.5 70.2 %copy-start.1 = (bf16[256,1024]{1,0:T(8,128)(2,1)S(1)}, bf16[256,1024]{1,0:T(8,128)(2,1)}, u32[]{:S(2)}) copy-start(bf16[256,1024]{1,0:T(8,128)(2,1)} %param.18) | copy-start | bytes 1572868
  93.1 69.9 %copy-start.2 = (bf16[256,1024]{1,0:T(8,128)(2,1)S(1)}, bf16[256,1024]{1,0:T(8,128)(2,1)}, u32[]{:S(2)}) copy-start(bf16[256,1024]{1,0:T(8,128)(2,1)} %param.17) | copy-start | bytes 1572868
  163.4 37.5 %copy-start.3 = (bf16[1024,256]{1,0:T(8,128)(2,1)S(1)}, bf16[1024,256]{1,0:T(8,128)(2,1)}, u32[]{:S(2)}) copy-start(bf16[1024,256]{1,0:T(8,128)(2,1)} %param.19) | copy-start | bytes 1572868
Sparse Core Ops, SparseCore 0:
  9.4 77.2 all-gather.1
where the time goes:
time: 227 us
  blocking collectives  138 us (61%)
  waiting for transfers between devices  63.9 us (28%)
  between operations  13.7 us (6%)
  matrix products  6.78 us (3%)
  other arithmetic  2.38 us (1%)
    all_to_all x8, blocking collectives, exchange(): return lax.all_to_all(blocks, axis, split_axis=0, concat_axis=0, tiled=True)  138 us
    all_gather x1, waiting for transfers between devices, on_device(): piece = lax.all_gather(frames, 'heads', axis=1, tiled=True)  63.2 us
  transfers between devices with their start and end apart: 1, of which 1 were waited for; matrix products, arithmetic and copies ran while one was open for 1% of the time, Pallas kernels for 0%

commit v1 on v0

--- a/solution.py
+++ b/solution.py
@@ -68,7 +68,10 @@
     local_query = jnp.dot(latents, w_query, preferred_element_type=F32).astype(BF16)
     queries = collect_rows(local_query, FRAMES)
     width = w_key.shape[1]
-    piece = lax.all_gather(frames, "heads", axis=1, tiled=True)
+    size = lax.axis_size("heads")
+    pieces = jnp.stack([frames for _ in range(size)])
+    pieces = lax.all_to_all(pieces, "heads", split_axis=0, concat_axis=0)
+    piece = jnp.concatenate(pieces, axis=1)
     keys = jnp.dot(piece, w_key, preferred_element_type=F32)
     values = jnp.dot(piece, w_value, preferred_element_type=F32)
     heads_here = width // HDIM

time: 227 us -> 268 us (1.18)
  waiting for transfers between devices: 63.9 us -> 104 us
  starting transfers between devices: 0.01 us -> 15.2 us
  between operations: 13.7 us -> 0.3 us
    all_to_all x0 -> x1, waiting for transfers between devices: none -> 104 us  [on_device(): pieces = lax.all_to_all(pieces, 'heads', split_axis=0, concat_axis=0)]
    all_gather x1 -> x0, waiting for transfers between devices: 63.2 us -> none  [on_device(): piece = lax.all_gather(frames, 'heads', axis=1, tiled=True)]
    all_to_all x0 -> x1, starting transfers between devices: none -> 15.2 us  [on_device(): pieces = lax.all_to_all(pieces, 'heads', split_axis=0, concat_axis=0)]
  transfers between devices with their start and end apart: 1 -> 1, of which waited for: 1 -> 1; matrix products, arithmetic and copies ran while one was open for 1% -> 0% of each run, Pallas kernels for 0% -> 0%
where the time goes in v1:
time: 268 us; the launch traced here: 267 us
  blocking collectives  136 us (51%)
  waiting for transfers between devices  104 us (39%)
  starting transfers between devices  15.2 us (6%)
  matrix products  5.18 us (2%)
  local copies, waits for them, and re-layouts  4.01 us (1%)
    all_to_all x8, blocking collectives, exchange(): return lax.all_to_all(blocks, axis, split_axis=0, concat_axis=0, tiled=True)  136 us
    all_to_all x1, waiting for transfers between devices, on_device(): pieces = lax.all_to_all(pieces, 'heads', split_axis=0, concat_axis=0)  104 us
    all_to_all x1, starting transfers between devices, on_device(): pieces = lax.all_to_all(pieces, 'heads', split_axis=0, concat_axis=0)  15.2 us
  transfers between devices with their start and end apart: 1, of which 1 were waited for; matrix products, arithmetic and copies ran while one was open for 0% of the time, Pallas kernels for 0%

profile of v1, /device:TPU:32, one launch (start us, length us, event | category | flops | bytes accessed | tf_op | source)
XLA Modules:
  0.0 267.1 jit_solution(16939593787214337827)
XLA Ops:
  0.0 1.3 convolution_convert_fusion.7
  1.4 14.9 %all_to_all.45 = bf16[32,8,256]{2,1,0:T(8,128)(2,1)S(1)} all-to-all(bf16[32,8,256]{2,1,0:T(8,128)(2,1)S(1)} %broadcast_in_dim.8), channel_id=1, replica_groups=mesh['frames_0'=4,'frames_1'=4,'frames_2'=2,'heads'=16] {'frames_0','fra..., dimensions={0} | all-to-all | bytes 262144 | tf_op jit(solution)/shard_map/all_to_all | solution.py:16
  16.3 2.6 stack.6
  18.9 15.2 %all-to-all-start = ((bf16[16,1024,72]{1,2,0:T(8,128)(2,1)}), bf16[16,1024,72]{1,2,0:T(8,128)(2,1)S(1)}, u32[]{:S(2)}, u32[]{:S(2)}) async-start(bf16[16,1024,72]{1,2,0:T(8,128)(2,1)} %stack.6), calls=%async_computation | async-start | bytes 4718592 | tf_op jit(solution)/shard_map/all_to_all | solution.py:73
  34.1 104.4 %all-to-all-done = bf16[16,1024,72]{1,2,0:T(8,128)(2,1)S(1)} async-done(((bf16[16,1024,72]{1,2,0:T(8,128)(2,1)}), bf16[16,1024,72]{1,2,0:T(8,128)(2,1)S(1)}, u32[]{:S(2)}, u32[]{:S(2)}) %all-to-all-start) | async-done | bytes 2359328 | tf_op jit(solution)/shard_map/all_to_all | solution.py:73
  138.5 0.9 convolution_convert_fusion.2
  139.4 0.2 copy-done.6
  139.6 0.9 convolution_convert_fusion.3
  140.5 0.5 bitcast_reduce_fusion
  141.0 0.4 fusion.2
  141.4 0.0 copy-start.4
  141.4 0.5 fusion.4
  141.9 0.0 copy-start.5
  141.9 0.0 copy-start.1
  141.9 0.1 copy.83
  142.1 0.2 copy.84
  142.3 0.2 reshape.194
  142.5 0.0 copy-start.2
  142.6 11.6 %all_to_all.46 = bf16[32,17,128]{2,1,0:T(8,128)(2,1)S(1)} all-to-all(bf16[32,17,128]{2,1,0:T(8,128)(2,1)S(1)} %pad_maximum_fusion), channel_id=1, replica_groups=mesh['frames_0'=4,'frames_1'=4,'frames_2'=2,'heads'=16] {'frames_0','fra..., dimensions={0} | all-to-all | bytes 278528 | tf_op jit(solution)/shard_map/all_to_all | solution.py:16
  154.2 0.1 copy.86
  154.4 0.1 fusion.32
  154.5 0.1 subtract_exponential_fusion
  154.6 0.2 fusion.20
  154.8 0.1 copy.92
  154.9 0.1 copy.87
  154.9 0.1 multiply_reduce_fusion.1
  155.1 0.1 fusion.19
  155.2 11.4 %all_to_all.47 = bf16[32,8,256]{2,1,0:T(8,128)(2,1)S(1)} all-to-all(bf16[32,8,256]{2,1,0:T(8,128)(2,1)S(1)} %broadcast_in_dim.9), channel_id=1, replica_groups=mesh['frames_0'=4,'frames_1'=4,'frames_2'=2,'heads'=16] {'frames_0','fra..., dimensions={0} | all-to-all | bytes 262144 | tf_op jit(solution)/shard_map/all_to_all | solution.py:16
  166.6 0.2 convolution_convert_fusion.5
  166.8 23.6 %all_to_all.48 = bf16[16,16,256]{2,1,0:T(8,128)(2,1)S(1)} all-to-all(bf16[16,16,256]{2,1,0:T(8,128)(2,1)S(1)} %bitcast.90), channel_id=1, replica_groups=mesh['frames_0'=4,'frames_1'=4,'frames_2'=2,'heads'=16] {'heads'}, dimensions={0} | all-to-all | bytes 262144 | tf_op jit(solution)/shard_map/all_to_all | solution.py:16
  190.5 19.1 %all_to_all.49 = bf16[16,16,256]{2,1,0:T(8,128)(2,1)S(1)} all-to-all(bf16[16,16,256]{2,1,0:T(8,128)(2,1)S(1)} %broadcast_in_dim.10), channel_id=1, replica_groups=mesh['frames_0'=4,'frames_1'=4,'frames_2'=2,'heads'=16] {'heads'}, dimensions={0} | all-to-all | bytes 262144 | tf_op jit(solution)/shard_map/all_to_all | solution.py:16
  209.6 0.1 multiply_reduce_fusion
  209.7 0.1 reduce_sum.79
  209.8 0.1 copy.93
  210.0 0.3 convolution_convert_fusion
  210.3 0.0 copy-done.2
  210.3 0.3 convolution_convert_fusion.1
  210.7 0.1 fusion.6
  210.7 0.0 copy-start.3
  210.8 22.0 %all_to_all.50 = bf16[32,8,2176]{2,1,0:T(8,128)(2,1)S(1)} all-to-all(bf16[32,8,2176]{2,1,0:T(8,128)(2,1)S(1)} %fusion.6), channel_id=1, replica_groups=mesh['frames_0'=4,'frames_1'=4,'frames_2'=2,'heads'=16] {'frames_0','fra..., dimensions={0} | all-to-all | bytes 2228224 | tf_op jit(solution)/shard_map/all_to_all | solution.py:16
  232.7 0.2 convert_reduce_fusion
  232.9 0.2 fusion.24
  233.1 0.1 fusion.16
  233.2 0.1 broadcast_in_dim.11
  233.3 15.0 %all_to_all.51 = bf16[32,8,1024]{2,1,0:T(8,128)(2,1)S(1)} all-to-all(bf16[32,8,1024]{2,1,0:T(8,128)(2,1)S(1)} %broadcast_in_dim.11), channel_id=1, replica_groups=mesh['frames_0'=4,'frames_1'=4,'frames_2'=2,'heads'=16] {'frames_0','fra..., dimensions={0} | all-to-all | bytes 1048576 | tf_op jit(solution)/shard_map/all_to_all | solution.py:16
  248.2 0.3 convolution_convert_fusion.4
  248.6 17.9 %all_to_all.52 = bf16[16,16,256]{2,1,0:T(8,128)(2,1)S(1)} all-to-all(bf16[16,16,256]{2,1,0:T(8,128)(2,1)S(1)} %bitcast.91), channel_id=1, replica_groups=mesh['frames_0'=4,'frames_1'=4,'frames_2'=2,'heads'=16] {'heads'}, dimensions={0} | all-to-all | bytes 262144 | tf_op jit(solution)/shard_map/all_to_all | solution.py:16
  266.5 0.6 add_convert_fusion
  (31 shorter events, 0.4 us)
Async XLA Ops:
  0.0 138.5 %copy-start = (bf16[1152,256]{1,0:T(8,128)(2,1)S(1)}, bf16[1152,256]{1,0:T(8,128)(2,1)}, u32[]{:S(2)}) copy-start(bf16[1152,256]{1,0:T(8,128)(2,1)} %param.13) | copy-start | bytes 1769476
  18.9 119.7 %all-to-all-start = ((bf16[16,1024,72]{1,2,0:T(8,128)(2,1)}), bf16[16,1024,72]{1,2,0:T(8,128)(2,1)S(1)}, u32[]{:S(2)}, u32[]{:S(2)}) async-start(bf16[16,1024,72]{1,2,0:T(8,128)(2,1)} %stack.6), calls=%async_computation | async-start | bytes 4718592 | tf_op jit(solution)/shard_map/all_to_all | solution.py:73
  138.5 1.1 copy-start.6
  141.4 25.3 %copy-start.4 = (bf16[256,256]{1,0:T(8,128)(2,1)S(1)}, bf16[256,256]{1,0:T(8,128)(2,1)}, u32[]{:S(2)}) copy-start(bf16[256,256]{1,0:T(8,128)(2,1)} %param.15) | copy-start | bytes 393220
  141.9 68.1 %copy-start.5 = (f32[256]{0:T(256)S(1)}, f32[256]{0:T(256)}, u32[]{:S(2)}) copy-start(f32[256]{0:T(256)} %param.16) | copy-start | bytes 3076
  141.9 68.1 %copy-start.1 = (bf16[256,1024]{1,0:T(8,128)(2,1)S(1)}, bf16[256,1024]{1,0:T(8,128)(2,1)}, u32[]{:S(2)}) copy-start(bf16[256,1024]{1,0:T(8,128)(2,1)} %param.18) | copy-start | bytes 1572868
  142.5 67.8 %copy-start.2 = (bf16[256,1024]{1,0:T(8,128)(2,1)S(1)}, bf16[256,1024]{1,0:T(8,128)(2,1)}, u32[]{:S(2)}) copy-start(bf16[256,1024]{1,0:T(8,128)(2,1)} %param.17) | copy-start | bytes 1572868
  210.7 37.5 %copy-start.3 = (bf16[1024,256]{1,0:T(8,128)(2,1)S(1)}, bf16[1024,256]{1,0:T(8,128)(2,1)}, u32[]{:S(2)}) copy-start(bf16[1024,256]{1,0:T(8,128)(2,1)} %param.19) | copy-start | bytes 1572868
